TPU v7x, 256 devices: a whole 4x4x8 slice. The times are simulated.
256 devices in a mesh: mode: 64 (over y, z, core), row: 4 (over x).
Axes of the slice: x: 4, y: 4, z: 8, core: 2. Of those that a mesh axis runs over, the one named last changes fastest.
Arguments:
- density: float32 [2, 2048, 2048], P(None, 'row', 'mode'), may hold values from -6 to 6
- auxiliary: float32 [2048, 256, 2, 128], P('row', 'mode'), may hold values from -2 to 2
- hamiltonian: bfloat16 [2048, 2048], P('row'), as said below
- coupling: int32 [2, 128], replicated, may hold values from 0 to 2047, as said below
- lead_index: int32 [256], P('mode'), may hold values from 0 to 1
- mode_level: float32 [256], P('mode'), may hold values from -2 to 2
- mode_width: float32 [256], P('mode'), may hold values from 0.05 to 3
- residue: float32 [256, 2], P('mode'), may hold values from -4 to 4
- occupation: float32 [256], P('mode'), may hold values from 0 to 1
- lead_gamma: bfloat16 [2, 128, 128], replicated, may hold values from -0.5 to 0.5
Outputs:
- density_rate: float32 [2, 2048, 2048], P(None, 'row', 'mode')
- auxiliary_rate: float32 [2048, 256, 2, 128], P('row', 'mode')
Inputs may be any that keep to these rules, and one draw needn't show every extreme that they name: `coupling`: all 256 entries are distinct orbitals. `hamiltonian`: Symmetric.
All inputs are finite; a program needn't handle non-finite values.
Results may differ from a plain program's by a relative error of at most 0.0044.
Values may be sent and summed in bfloat16 or wider, within the bound.
A program may use at most 128 MiB of HBM per device.

v0:
```python
import jax
import jax.numpy as jnp
from jax import lax
from jax.sharding import PartitionSpec as P

H2 = 0.05
F32 = jnp.float32
BF = jnp.bfloat16


def dot(a, b, ca=1, cb=0):
    return lax.dot_general(a, b, (((ca,), (cb,)), ((), ())), preferred_element_type=F32)


def over_row(x):
    devices = lax.axis_size("row")
    return lax.all_to_all(jnp.broadcast_to(x[None], (devices, *x.shape)), "row", 0, 0, tiled=True)


def by_lead(x, gamma):
    leads, coupled = gamma.shape[:2]
    return jnp.concatenate(
        [dot(x[:, l * coupled : (l + 1) * coupled], gamma[l]) for l in range(leads)], axis=1
    )


def shards(
    density,
    auxiliary,
    hamiltonian,
    coupling,
    lead_index,
    mode_level,
    mode_width,
    residue,
    occupation,
    lead_gamma,
):
    rows, cols = density.shape[1:]
    n = hamiltonian.shape[1]
    leads, coupled = coupling.shape
    q = leads * coupled
    modes = auxiliary.shape[1]
    n_mode = lax.axis_size("mode")
    n_row = lax.axis_size("row")
    x_pos, m_pos = (lax.axis_index("row"), lax.axis_index("mode"))
    row_start, col_start = (x_pos * rows, m_pos * cols)
    flat = coupling.reshape(-1)
    e_full = (jnp.arange(n, dtype=jnp.int32)[:, None] == flat[None, :]).astype(BF)
    e_row = (row_start + jnp.arange(rows, dtype=jnp.int32)[:, None] == flat[None, :]).astype(BF)
    e_col = (col_start + jnp.arange(cols, dtype=jnp.int32)[:, None] == flat[None, :]).astype(BF)
    g_row = by_lead(e_row, lead_gamma).astype(BF)
    g_col = by_lead(e_col, lead_gamma).astype(BF)
    rho_t = jnp.swapaxes(density, 1, 2).astype(BF).reshape(2 * cols, rows)
    ham_ct = jnp.swapaxes(lax.dynamic_slice_in_dim(hamiltonian, col_start, cols, 1), 0, 1)
    first = over_row(jnp.concatenate([ham_ct, rho_t], axis=0))
    first = jnp.moveaxis(first, 0, 1).reshape(3 * cols, n)
    ham_c = first[:cols]
    applied = dot(first, hamiltonian, 1, 1)
    ham2_ct = applied[:cols].astype(BF)
    hrho_t = applied[cols:]
    he_row = dot(hamiltonian, e_full)
    hg_row = by_lead(he_row.astype(BF), lead_gamma)
    he_col = dot(ham_c, e_full).astype(BF)
    hg_col = by_lead(he_col, lead_gamma)
    panel = lax.all_gather(rho_t.reshape(2, cols, rows), "mode", axis=1, tiled=True)
    ham2_all = lax.all_gather(ham2_ct, "mode", axis=0, tiled=True)
    pi_b = auxiliary.astype(BF).reshape(rows, modes * 2 * coupled)
    pi_all = lax.all_gather(pi_b, "row", axis=0, tiled=True)
    onehot = (lead_index[:, None] == jnp.arange(leads, dtype=jnp.int32)[None, :]).astype(F32)
    lam_re, lam_im = (-mode_width, mode_level)
    l_parts, m_parts = ([[], []], [[], []])
    for l in range(leads):
        s = [sum((onehot[k, l] * auxiliary[:, k, p] for k in range(modes))) for p in range(2)]
        m_re = sum(
            (
                onehot[k, l] * (lam_re[k] * auxiliary[:, k, 0] - lam_im[k] * auxiliary[:, k, 1])
                for k in range(modes)
            )
        )
        m_im = sum(
            (
                onehot[k, l] * (lam_re[k] * auxiliary[:, k, 1] + lam_im[k] * auxiliary[:, k, 0])
                for k in range(modes)
            )
        )
        for p in range(2):
            l_parts[p].append(s[p])
        m_parts[0].append(m_re)
        m_parts[1].append(m_im)
    l_part = jnp.concatenate(l_parts[0] + l_parts[1], axis=1)
    m_part = jnp.concatenate(m_parts[0] + m_parts[1], axis=1)
    w_l = jnp.concatenate([(residue[:, p][:, None] * onehot).sum(0) for p in range(2)])
    v_l = jnp.concatenate(
        [((residue[:, p] * occupation)[:, None] * onehot).sum(0) for p in range(2)]
    )
    hrho_b = hrho_t.astype(BF)
    f_re = dot(
        jnp.concatenate([hrho_b[cols:], rho_t[cols:]], 0),
        jnp.concatenate([2 * g_col, -hg_col.astype(BF)], 0),
        0,
        0,
    )
    f_im = dot(
        jnp.concatenate([hrho_b[:cols], rho_t[:cols]], 0),
        jnp.concatenate([-2 * g_col, hg_col.astype(BF)], 0),
        0,
        0,
    )
    f_part = jnp.concatenate([f_re, f_im], axis=1)
    l_part_b = l_part.astype(BF)
    n_part = jnp.concatenate(
        [dot(l_part_b[:, :q], g_row, 0, 0), -dot(l_part_b[:, q:], g_row, 0, 0)], axis=1
    )
    piece = rows // n_mode
    n_piece = q // n_mode
    scal = jnp.concatenate([w_l, v_l])
    scal = jnp.zeros((n_mode, 1, 2 * q), F32).at[:, 0, : scal.shape[0]].set(scal)
    payload = jnp.concatenate(
        [a.reshape(n_mode, -1, 2 * q) for a in (l_part, m_part, f_part, n_part)] + [scal], axis=1
    )
    mine = lax.psum_scatter(payload, "mode", scatter_dimension=0, tiled=True)[0]
    n_mine = over_row(mine[3 * piece : 3 * piece + n_piece]).sum(0)
    w_sum, v_sum = (mine[-1, : 2 * leads], mine[-1, 2 * leads : 4 * leads])
    mine = jnp.concatenate([mine[: 3 * piece], n_mine], axis=0).astype(BF)
    whole = lax.all_gather(mine, "mode", axis=0, tiled=False)
    l1_b = whole[:, :piece].reshape(rows, 2 * q)
    m1 = whole[:, piece : 2 * piece].reshape(rows, 2 * q).astype(F32)
    f_all = whole[:, 2 * piece : 3 * piece].reshape(rows, 2 * q).astype(F32)
    n_all = whole[:, 3 * piece :].reshape(q, 2 * q)
    grow_full = by_lead(e_full, lead_gamma).astype(BF)
    src = jnp.concatenate([dot(panel[p], grow_full, 0, 0) for p in range(2)], axis=1)
    w_q = jnp.repeat(w_sum, coupled)
    v_q = jnp.repeat(v_sum, coupled)
    s_re, s_im = (src[:, :q], src[:, q:])
    g_row_f = g_row.astype(F32)
    drive = jnp.concatenate(
        [
            w_q[:q] * s_re - w_q[q:] * s_im - (v_q[:q] - v_q[q:]) * g_row_f,
            w_q[:q] * s_im + w_q[q:] * s_re - (v_q[:q] + v_q[q:]) * g_row_f,
        ],
        axis=1,
    )
    x_row = (3.0 * l1_b.astype(F32) + 2 * H2 * (m1 + drive)).astype(BF)
    p1 = jnp.concatenate([dot(e_col, l1_b[:, p * q : (p + 1) * q], 1, 1) for p in range(2)], 0)
    xe = jnp.concatenate([dot(e_col, x_row[:, p * q : (p + 1) * q], 1, 1) for p in range(2)], 0)
    rhoh_t = jnp.concatenate([dot(ham_c, panel[p]) for p in range(2)], 0)
    y = hrho_t - 2.0 * rhoh_t + 2.0 * jnp.concatenate([-p1[cols:], p1[:cols]], 0)
    z = dot(lax.dynamic_slice_in_dim(ham_c, row_start, rows, 1), l1_b)
    owner = col_start // rows
    own_l = lax.dynamic_slice_in_dim(l1_b, col_start - owner * rows, cols, 0)
    own_x = lax.dynamic_slice_in_dim(x_row, col_start - owner * rows, cols, 0)
    mask = (x_pos == owner).astype(BF)
    second = over_row(jnp.concatenate([y.astype(BF), ham2_ct], 0))
    second = jnp.moveaxis(second, 0, 1).reshape(3 * cols, n)
    third = (
        over_row(jnp.concatenate([z.astype(BF), own_l * mask, own_x * mask], 0)).astype(F32).sum(0)
    )
    z, l_c, x_c = (third[:cols], third[cols : 2 * cols], third[2 * cols :])
    hy = dot(second[: 2 * cols], hamiltonian, 1, 1)
    ham2_c = second[2 * cols :]
    rhoh2_t = jnp.concatenate([dot(ham2_c, panel[p]) for p in range(2)], 0)
    b_re = x_c[:, :q] + 4 * H2 * z[:, q:]
    b_im = -x_c[:, q:] + 4 * H2 * z[:, :q]
    back_re = dot(b_re.astype(BF), e_row, 1, 1)
    back_im = dot(b_im.astype(BF), e_row, 1, 1)
    l_cb = l_c.astype(BF)
    he_row_b = he_row.astype(BF)
    c1_re, c1_im = (dot(l_cb[:, :q], he_row_b, 1, 1), -dot(l_cb[:, q:], he_row_b, 1, 1))
    c2_re, c2_im = (dot(he_col, l1_b[:, :q], 1, 1), dot(he_col, l1_b[:, q:], 1, 1))
    d_re, d_im = (c1_re - c2_re, c1_im - c2_im)
    comm = hrho_t - rhoh_t
    base = -2 * H2 * (hy + rhoh2_t) + xe
    out_re = 3.0 * comm[cols:] + base[:cols] + back_re + 2 * H2 * d_im
    out_im = -3.0 * comm[:cols] + base[cols:] + back_im - 2 * H2 * d_re
    density_rate = jnp.swapaxes(jnp.stack([out_re, out_im]), 1, 2)
    h_pi = dot(hamiltonian, pi_all).reshape(rows, modes, 2, coupled)
    h2_pi = dot(ham2_all, pi_all.reshape(n, -1), 0, 0).reshape(rows, modes, 2, coupled)
    lg = jnp.concatenate([by_lead(l1_b[:, p * q : (p + 1) * q], lead_gamma) for p in range(2)], 1)
    u = 2 * H2 * (f_all + lg + dot(e_row, n_all))
    outs = []
    for k in range(modes):
        is0 = onehot[k, 0] > 0

        def pick(a):
            return jnp.where(is0, a[:, :coupled], a[:, coupled:])

        lr, li = (lam_re[k], lam_im[k])
        wr, wi, occ = (residue[k, 0], residue[k, 1], occupation[k])
        sr, si, ur, ui = (pick(s_re), pick(s_im), pick(u[:, :q]), pick(u[:, q:]))
        gk, hgk = (pick(g_row_f), pick(hg_row))
        br, bi = (sr - occ * gk, si - occ * gk)
        ar, ai = (3 + 2 * H2 * lr, 2 * H2 * li)
        tr = ar * br - ai * bi + ur - 2 * H2 * occ * hgk
        ti = ar * bi + ai * br + ui + 2 * H2 * occ * hgk
        pr, pim = (auxiliary[:, k, 0], auxiliary[:, k, 1])
        cr = 3 * lr + 2 * H2 * (lr * lr - li * li)
        ci = 3 * li + 4 * H2 * lr * li
        er, ei = (4 * H2 * li, -3 - 4 * H2 * lr)
        hr, hi = (h_pi[:, k, 0], h_pi[:, k, 1])
        outs.append(
            cr * pr - ci * pim + er * hr - ei * hi - 2 * H2 * h2_pi[:, k, 0] + wr * tr - wi * ti
        )
        outs.append(
            cr * pim + ci * pr + er * hi + ei * hr - 2 * H2 * h2_pi[:, k, 1] + wr * ti + wi * tr
        )
    auxiliary_rate = jnp.stack(outs, axis=1).reshape(rows, modes, 2, coupled)
    return (density_rate, auxiliary_rate)


def solution(mesh):
    in_specs = (
        P(None, "row", "mode"),
        P("row", "mode", None, None),
        P("row", None),
        P(),
        P("mode"),
        P("mode"),
        P("mode"),
        P("mode", None),
        P("mode"),
        P(),
    )
    out_specs = (P(None, "row", "mode"), P("row", "mode", None, None))
    return jax.shard_map(shards, mesh=mesh, in_specs=in_specs, out_specs=out_specs, check_vma=False)
```

profile of v0, /device:TPU:1, one launch (start us, length us, event | category | flops | bytes accessed | tf_op | source)
XLA Modules:
  0.0 596.0 jit_solution(17959333989548009049)
XLA Ops:
  9.8 4.8 all-to-all-start
  14.7 4.1 fusion.164
  21.0 6.2 %convert_bitcast_fusion.1 = (bf16[512,128]{1,0:T(8,128)(2,1)}, f32[512,1,1,128]{3,0,2,1:T(8,128)}, bf16[512,128]{1,0:T(8,128)(2,1)}, f32[512,1,1,128]{3,0,2,1:T(...) fusion(f32[512,1,1,128]{3,0,2,1:T(8,128)S(1)} %bitcast.292, ...), kind=kLoop, calls=%fused_computation.175 | loop fusion | flops 2097152 | bytes 3670048 | tf_op jit(solution)/shard_map/add | solution.py:74
  27.2 8.4 %add_bitcast_fusion = f32[64,8,128]{2,1,0:T(8,128)} fusion(f32[]{:T(128)} %bitcast.15, f32[]{:T(128)} %bitcast.14, f32[]{:T(128)} %bitcast.13, f32[]{:T(128)} %bitcast.12, f32[512,1,1,128]{3,0,2,1:T(8,128)S(1)} %bitcast.272, f32[]{:T(128)} %bitcast.20, f32[512,1,1,128]{3,0,2,1:T(8,128)S(1)} %bitcast.279, f32[]{:T(128)} %bitcast.19, ...), kind=kLoop, calls=%fused_computation.101 | loop fusion | flops 1245184 | bytes 2359344 | tf_op jit(solution)/shard_map/add | solution.py:81
  35.6 8.4 %add_bitcast_fusion.1 = f32[64,8,128]{2,1,0:T(8,128)} fusion(f32[]{:T(128)} %bitcast.10, f32[]{:T(128)} %bitcast.9, f32[]{:T(128)} %bitcast.8, f32[]{:T(128)} %bitcast.7, f32[512,1,1,128]{3,0,2,1:T(8,128)S(1)} %bitcast.273, f32[]{:T(128)} %bitcast.20, f32[512,1,1,128]{3,0,2,1:T(8,128)S(1)} %bitcast.280, f32[]{:T(128)} %bitcast.19, ...), kind=kLoop, calls=%fused_computation.102 | loop fusion | flops 1245184 | bytes 2359344 | tf_op jit(solution)/shard_map/add | solution.py:81
  44.1 8.5 %add_bitcast_fusion.2 = f32[64,8,128]{2,1,0:T(8,128)} fusion(f32[]{:T(128)} %bitcast.15, f32[]{:T(128)} %bitcast.14, f32[]{:T(128)} %bitcast.13, f32[]{:T(128)} %bitcast.12, f32[512,1,1,128]{3,0,2,1:T(8,128)S(1)} %bitcast.281, f32[]{:T(128)} %bitcast.20, f32[512,1,1,128]{3,0,2,1:T(8,128)S(1)} %bitcast.274, f32[]{:T(128)} %bitcast.19, ...), kind=kLoop, calls=%fused_computation.103 | loop fusion | flops 1245184 | bytes 2359344 | tf_op jit(solution)/shard_map/add | solution.py:75
  52.6 8.4 %add_bitcast_fusion.3 = f32[64,8,128]{2,1,0:T(8,128)} fusion(f32[]{:T(128)} %bitcast.10, f32[]{:T(128)} %bitcast.9, f32[]{:T(128)} %bitcast.8, f32[]{:T(128)} %bitcast.7, f32[512,1,1,128]{3,0,2,1:T(8,128)S(1)} %bitcast.282, f32[]{:T(128)} %bitcast.20, f32[512,1,1,128]{3,0,2,1:T(8,128)S(1)} %bitcast.275, f32[]{:T(128)} %bitcast.19, ...), kind=kLoop, calls=%fused_computation.104 | loop fusion | flops 1245184 | bytes 2359344 | tf_op jit(solution)/shard_map/add | solution.py:75
  67.0 2.1 copy.205
  69.0 2.0 reshape.500
  71.1 2.3 pad_maximum_fusion
  80.8 2.5 copy.202
  84.1 13.7 %concatenate.113 = f32[64,29,512]{2,1,0:T(8,128)} concatenate(f32[64,8,512]{2,1,0:T(8,128)} %pad_maximum_fusion, f32[64,8,512]{2,1,0:T(8,128)} %pad_maximum_fusion.1, f32[64,8,512]{2,1,0:T(8,128)} %bitcast.327, f32[64,4,512]{2,1,0:T(4,128)} %reshape.500, f32[64,1,512]{2,1,0:T(1,128)} %scatter.8), dimensions={1} | concatenate | bytes 7602176 | tf_op jit(solution)/shard_map/concatenate | solution.py:119
  97.8 1.4 slice.1048
  99.4 3.3 convert_element_type.100
  102.6 2.6 reshape.502
  137.6 1.8 fusion.161
  144.5 96.6 %reduce-scatter.2.cloned.1.call-done = f32[1,29,512]{2,1,0:T(8,128)} async-done(((f32[64,29,512]{2,1,0:T(8,128)}), f32[1,29,512]{2,1,0:T(8,128)}) %reduce-scatter.2.cloned.1.call-update) | async-done | bytes 59408 | tf_op jit(solution)/shard_map/reduce_scatter | solution.py:122
  242.4 3.8 all-to-all-start.1
  251.2 74.0 %all-gather.11.cloned.1.call-done = bf16[2048,512]{1,0:T(8,128)(2,1)} async-done(((bf16[32,512]{1,0:T(8,128)(2,1)}), bf16[2048,512]{1,0:T(8,128)(2,1)}) %all-gather.11.cloned.1.call-update) | async-done | bytes 2097168 | tf_op jit(solution)/shard_map/all_gather | solution.py:67
  325.2 49.4 %all-gather.9.cloned.1.call-done = bf16[2048,1024]{1,0:T(8,128)(2,1)} async-done(((bf16[512,1024]{1,0:T(8,128)(2,1)}), bf16[2048,1024]{1,0:T(8,128)(2,1)}) %all-gather.9.cloned.1.call-update) | async-done | bytes 4194320 | tf_op jit(solution)/shard_map/all_gather | solution.py:69
  374.6 5.2 fusion.173
  381.2 1.8 copy.253
  383.0 4.6 fusion.172
  387.5 1.4 fusion.163
  388.9 1.8 copy.252
  390.7 1.8 copy.251
  392.5 1.8 copy.254
  394.3 1.8 copy.257
  396.1 1.8 copy.256
  397.9 1.8 copy.255
  399.7 1.8 copy.258
  401.5 1.8 copy.261
  403.3 1.8 copy.260
  405.0 1.8 copy.259
  406.8 1.8 copy.262
  408.6 1.8 copy.265
  410.4 1.8 copy.264
  412.2 1.8 copy.263
  414.0 1.8 copy.266
  415.8 41.6 %all-gather.5.cloned.1.call-done = bf16[2,2048,512]{2,1,0:T(8,128)(2,1)} async-done(((bf16[2,32,512]{2,1,0:T(8,128)(2,1)}), bf16[2,2048,512]{2,1,0:T(8,128)(2,1)}) %all-gather.5.cloned.1.call-update) | async-done | bytes 4194320 | tf_op jit(solution)/shard_map/all_gather | solution.py:66
  457.5 3.0 fusion.8
  460.5 2.8 select_subtract_fusion.1
  463.3 2.0 multiply_subtract_fusion.1
  465.3 2.8 select_subtract_fusion
  468.1 1.6 select_subtract_fusion.5
  471.8 62.8 %all-gather.7.cloned.1.call-done = bf16[64,28,512]{2,1,0:T(8,128)(2,1)} async-done(((bf16[1,28,512]{2,1,0:T(8,128)(2,1)}), bf16[64,28,512]{2,1,0:T(8,128)(2,1)}) %all-gather.7.cloned.1.call-update) | async-done | bytes 1835024 | tf_op jit(solution)/shard_map/all_gather | solution.py:126
  536.3 1.5 fusion.21
  544.3 4.3 all-to-all-start.2
  548.6 1.8 slice.780
  550.4 1.7 reshape.505
  552.2 1.9 fusion.6
  554.3 1.7 bitcast_dynamic-update-slice_fusion.7
  556.0 1.4 bitcast_dynamic-update-slice_fusion.6
  557.5 1.5 bitcast_dynamic-update-slice_fusion.5
  559.1 1.5 bitcast_dynamic-update-slice_fusion.4
  560.6 1.5 bitcast_dynamic-update-slice_fusion.3
  562.2 1.4 bitcast_dynamic-update-slice_fusion.2
  563.6 1.5 bitcast_dynamic-update-slice_fusion.1
  565.2 1.4 bitcast_dynamic-update-slice_fusion
  566.6 2.9 copy.232
  572.5 4.0 all-to-all-start.3
  577.4 1.7 slice_bitcast_fusion.15
  579.1 4.3 all-to-all-done.3
  584.5 2.4 fusion.4
  (290 shorter events, 51.3 us)
Async XLA Ops:
  7.2 7.5 %copy-start.51 = (f32[2,512,32]{1,2,0:T(8,128)S(1)}, f32[2,512,32]{1,2,0:T(8,128)}, u32[]{:S(2)}) copy-start(f32[2,512,32]{1,2,0:T(8,128)} %param.12) | copy-start | bytes 393220
  9.8 65.5 %all-to-all-start = ((bf16[4,96,512]{2,1,0:T(8,128)(2,1)}), bf16[4,96,512]{2,1,0:T(8,128)(2,1)}, u32[]{:S(2)}, u32[]{:S(2)}) async-start(bf16[4,96,512]{2,1,0:T(8,128)(2,1)} %broadcast_in_dim.18), calls=%async_computation | async-start | bytes 786432 | tf_op jit(solution)/shard_map/all_to_all | solution.py:17
  14.6 226.4 %reduce-scatter.2.cloned.1.call-start = ((), (), s32[]{:S(2)}) async-start(), calls=%async_computation.6 | async-start | bytes 4259840 | tf_op jit(solution)/shard_map/reduce_scatter | solution.py:122
  14.7 60.0 %copy-start.48 = (bf16[2,32,512]{2,1,0:T(8,128)(2,1)}, bf16[2,32,512]{2,1,0:T(8,128)(2,1)S(1)}, u32[]{:S(2)}) copy-start(bf16[2,32,512]{2,1,0:T(8,128)(2,1)S(1)} %convert_bitcast_fusion.5) | copy-start | bytes 196612
  14.7 4.1 copy-start.82
  14.7 5.0 copy-start.81
  14.7 5.7 copy-start.85
  18.8 33.8 %copy-start.1 = (f32[512,1,1,128]{3,2,1,0:T(1,128)}, f32[512,1,1,128]{3,2,1,0:T(1,128)S(1)}, u32[]{:S(2)}) copy-start(f32[512,1,1,128]{3,2,1,0:T(1,128)S(1)} %get-tuple-element.71) | copy-start | bytes 786436
  18.8 33.8 %copy-start.3 = (f32[512,1,1,128]{3,2,1,0:T(1,128)}, f32[512,1,1,128]{3,2,1,0:T(1,128)S(1)}, u32[]{:S(2)}) copy-start(f32[512,1,1,128]{3,2,1,0:T(1,128)S(1)} %get-tuple-element.68) | copy-start | bytes 786436
  18.8 33.7 %copy-start.5 = (f32[512,1,1,128]{3,2,1,0:T(1,128)}, f32[512,1,1,128]{3,2,1,0:T(1,128)S(1)}, u32[]{:S(2)}) copy-start(f32[512,1,1,128]{3,2,1,0:T(1,128)S(1)} %get-tuple-element.72) | copy-start | bytes 786436
  44.1 17.4 %copy-start.65 = (s32[2,128]{1,0:T(2,128)S(1)}, s32[2,128]{1,0:T(2,128)}, u32[]{:S(2)}) copy-start(s32[2,128]{1,0:T(2,128)} %param.15) | copy-start | bytes 3076
  44.1 17.5 %copy-start.24 = (bf16[2,128,128]{2,1,0:T(8,128)(2,1)S(1)}, bf16[2,128,128]{2,1,0:T(8,128)(2,1)}, u32[]{:S(2)}) copy-start(bf16[2,128,128]{2,1,0:T(8,128)(2,1)} %param.21) | copy-start | bytes 196612
  64.9 6.2 %copy-start.71 = (f32[4,2]{0,1:T(2,128)S(1)}, f32[4,2]{0,1:T(2,128)}, u32[]{:S(2)}) copy-start(f32[4,2]{0,1:T(2,128)} %param.19) | copy-start | bytes 100
  64.9 6.2 %copy-start.80 = (f32[4]{0:T(128)S(1)}, f32[4]{0:T(128)}, u32[]{:S(2)}) copy-start(f32[4]{0:T(128)} %param.20) | copy-start | bytes 52
  71.0 2.4 copy-start.33
  71.0 2.4 copy-start.34
  71.0 2.4 copy-start.35
  71.0 2.4 copy-start.36
  76.2 2.7 copy-start.75
  76.3 2.7 copy-start.76
  77.0 2.5 copy-start.58
  97.8 227.4 %all-gather.11.cloned.1.call-start = ((), (), s32[]{:S(2)}) async-start(), calls=%async_computation.9 | async-start | bytes 2129920 | tf_op jit(solution)/shard_map/all_gather | solution.py:67
  99.3 275.3 %all-gather.9.cloned.1.call-start = ((), (), s32[]{:S(2)}) async-start(), calls=%async_computation.8 | async-start | bytes 5242880 | tf_op jit(solution)/shard_map/all_gather | solution.py:69
  105.2 352.2 %all-gather.5.cloned.1.call-start = ((), (), s32[]{:S(2)}) async-start(), calls=%async_computation.5 | async-start | bytes 4259840 | tf_op jit(solution)/shard_map/all_gather | solution.py:66
  242.4 8.1 %all-to-all-start.1 = ((f32[4,4,512]{2,1,0:T(4,128)}), f32[4,4,512]{2,1,0:T(4,128)S(1)}, u32[]{:S(2)}, u32[]{:S(2)}) async-start(f32[4,4,512]{2,1,0:T(4,128)} %broadcast_in_dim.20), calls=%async_computation.2 | async-start | bytes 65536 | tf_op jit(solution)/shard_map/all_to_all | solution.py:17
  246.2 288.4 %all-gather.7.cloned.1.call-start = ((), (), s32[]{:S(2)}) async-start(), calls=%async_computation.7 | async-start | bytes 2129920 | tf_op jit(solution)/shard_map/all_gather | solution.py:126
  415.8 47.4 %copy-start.86 = (f32[256]{0:T(256)S(1)}, f32[256]{0:T(256)}, u32[]{:S(2)}) copy-start(f32[256]{0:T(256)} %broadcast_bitcast_fusion.1) | copy-start | bytes 3076
  415.8 47.4 %copy-start.87 = (f32[256]{0:T(256)S(1)}, f32[256]{0:T(256)}, u32[]{:S(2)}) copy-start(f32[256]{0:T(256)} %broadcast_bitcast_fusion.2) | copy-start | bytes 3076
  415.8 47.4 %copy-start.88 = (f32[256]{0:T(256)S(1)}, f32[256]{0:T(256)}, u32[]{:S(2)}) copy-start(f32[256]{0:T(256)} %broadcast_bitcast_fusion.3) | copy-start | bytes 3076
  415.8 47.4 %copy-start.89 = (f32[256]{0:T(256)S(1)}, f32[256]{0:T(256)}, u32[]{:S(2)}) copy-start(f32[256]{0:T(256)} %broadcast_bitcast_fusion) | copy-start | bytes 3076
  457.5 3.0 copy-start.9
  457.5 5.8 copy-start.62
  457.5 5.8 copy-start.64
  457.5 5.8 copy-start.83
  457.5 5.8 copy-start.90
  457.5 5.8 copy-start.91
  465.3 4.3 copy-start.57
  470.7 65.1 %copy-start.78 = (s32[32]{0:T(128)S(1)}, s32[32]{0:T(128)}, u32[]{:S(2)}) copy-start(s32[32]{0:T(128)} %copy-done.77) | copy-start | bytes 388
  471.8 66.7 %copy-start.66 = (s32[2,128]{1,0:T(2,128)S(1)}, s32[2,128]{1,0:T(2,128)}, u32[]{:S(2)}) copy-start(s32[2,128]{1,0:T(2,128)} %param.15) | copy-start | bytes 3076
  535.8 6.1 %copy-start.7 = (bf16[512,512]{1,0:T(8,128)(2,1)}, bf16[512,512]{1,0:T(8,128)(2,1)S(1)}, u32[]{:S(2)}) copy-start(bf16[512,512]{1,0:T(8,128)(2,1)S(1)} %slice_bitcast_fusion.14) | copy-start | bytes 1572868
  536.2 6.6 %copy-start.47 = (f32[96,512]{1,0:T(8,128)S(1)}, f32[96,512]{1,0:T(8,128)}, u32[]{:S(2)}) copy-start(f32[96,512]{1,0:T(8,128)} %copy-done.46) | copy-start | bytes 589828
  536.2 6.6 %copy-start.69 = (f32[32,512]{1,0:T(8,128)S(1)}, f32[32,512]{1,0:T(8,128)}, u32[]{:S(2)}) copy-start(f32[32,512]{1,0:T(8,128)} %fusion.5) | copy-start | bytes 196612
  536.3 6.6 %copy-start.70 = (f32[32,512]{1,0:T(8,128)S(1)}, f32[32,512]{1,0:T(8,128)}, u32[]{:S(2)}) copy-start(f32[32,512]{1,0:T(8,128)} %fusion.2) | copy-start | bytes 196612
  536.3 7.2 %copy-start.53 = (bf16[32,512]{1,0:T(8,128)(2,1)S(1)}, bf16[32,512]{1,0:T(8,128)(2,1)}, u32[]{:S(2)}) copy-start(bf16[32,512]{1,0:T(8,128)(2,1)} %slice.1048) | copy-start | bytes 98308
  537.8 5.0 copy-start.22
  540.2 12.0 %copy-start.73 = (s32[512]{0:T(512)S(1)}, s32[512]{0:T(512)}, u32[]{:S(2)}) copy-start(s32[512]{0:T(512)} %copy-done.72) | copy-start | bytes 6148
  544.3 27.4 %all-to-all-start.2 = ((bf16[4,96,512]{2,1,0:T(8,128)(2,1)}), bf16[4,96,512]{2,1,0:T(8,128)(2,1)}, u32[]{:S(2)}, u32[]{:S(2)}) async-start(bf16[4,96,512]{2,1,0:T(8,128)(2,1)} %broadcast_in_dim.21), calls=%async_computation.3 | async-start | bytes 786432 | tf_op jit(solution)/shard_map/all_to_all | solution.py:17
  554.2 3.2 copy-start.4
  554.2 3.2 copy-start.6
  554.2 3.2 copy-start.20
  554.2 3.2 copy-start.21
  554.2 3.2 copy-start.39
  554.3 3.2 copy-start.44
  554.3 3.2 copy-start.45
  566.6 4.3 copy-start.60
  566.6 4.3 copy-start.23
  566.6 4.3 copy-start.67
  566.6 4.3 copy-start.79
  569.5 13.9 %copy-start.15 = (bf16[256,512]{1,0:T(8,128)(2,1)S(1)}, bf16[256,512]{1,0:T(8,128)(2,1)}, u32[]{:S(2)}) copy-start(bf16[256,512]{1,0:T(8,128)(2,1)} %copy-done.13) | copy-start | bytes 786436
  570.9 12.9 %copy-start.8 = (bf16[512,512]{1,0:T(8,128)(2,1)S(1)}, bf16[512,512]{1,0:T(8,128)(2,1)}, u32[]{:S(2)}) copy-start(bf16[512,512]{1,0:T(8,128)(2,1)} %copy-done.7) | copy-start | bytes 1572868
  572.5 10.8 %all-to-all-start.3 = ((bf16[4,96,512]{2,1,0:T(8,128)(2,1)}), bf16[4,96,512]{2,1,0:T(8,128)(2,1)S(1)}, u32[]{:S(2)}, u32[]{:S(2)}) async-start(bf16[4,96,512]{2,1,0:T(8,128)(2,1)} %broadcast_in_dim.26), calls=%async_computation.4 | async-start | bytes 786432 | tf_op jit(solution)/shard_map/all_to_all | solution.py:17
  583.6 3.3 copy-start.84
  584.5 2.9 copy-start.54
  584.5 2.9 copy-start.55
  (37 other events, 56.2 us)
Sparse Core Ops, SparseCore 0:
  97.9 143.1 reduce-scatter.1
  243.9 81.2 all-gather.10
  327.0 47.5 all-gather.8
  377.3 80.1 all-gather.4
  460.1 74.4 all-gather.6
where the time goes:
time: 599 us; the launch traced here: 596 us
  waiting for transfers between devices  329 us (55%)
  local copies, waits for them, and re-layouts  86.9 us (15%)
  other arithmetic  74.6 us (12%)
  between operations  45.6 us (8%)
  matrix products  42.4 us (7%)
  starting transfers between devices  17.1 us (3%)
    reduce_scatter x1, waiting for transfers between devices, shards(): mine = lax.psum_scatter(payload, 'mode', scatter_dimension=0, tiled=True)[0]  96.6 us
    all_gather x1, waiting for transfers between devices, shards(): ham2_all = lax.all_gather(ham2_ct, 'mode', axis=0, tiled=True)  74 us
    all_gather x1, waiting for transfers between devices, shards(): whole = lax.all_gather(mine, 'mode', axis=0, tiled=False)  62.8 us
    all_gather x1, waiting for transfers between devices, shards(): pi_all = lax.all_gather(pi_b, 'row', axis=0, tiled=True)  49.4 us
    dot_general x42, matrix products, dot(): lax.dot_general(a, b, (((ca,), (cb,)), ((), ())), preferred_element_type=...  42.4 us
    all_gather x1, waiting for transfers between devices, shards(): lax.all_gather(rho_t.reshape(2, cols, rows), 'mode', axis=1, tiled=True)  41.6 us
    unnamed x204, local copies, waits for them, and re-layouts  38 us
    all_to_all x4, starting transfers between devices, over_row(): lax.all_to_all(jnp.broadcast_to(x[None], (devices, *x.shape)), 'row', 0,...  17 us
  transfers between devices with their start and end apart: 9, of which 6 were waited for; matrix products, arithmetic and copies ran while one was open for 27% of the time, Pallas kernels for 0%

commit v1 on v0

--- a/solution.py
+++ b/solution.py
@@ -6,6 +6,12 @@
 H2 = 0.05
 F32 = jnp.float32
 BF = jnp.bfloat16
+
+
+def laid_out(blocks, dim):
+    blocks = jnp.moveaxis(blocks, 0, dim)
+    shape = blocks.shape
+    return blocks.reshape(*shape[:dim], shape[dim] * shape[dim + 1], *shape[dim + 2 :])
 
 
 def dot(a, b, ca=1, cb=0):
@@ -66,7 +72,19 @@
     panel = lax.all_gather(rho_t.reshape(2, cols, rows), "mode", axis=1, tiled=True)
     ham2_all = lax.all_gather(ham2_ct, "mode", axis=0, tiled=True)
     pi_b = auxiliary.astype(BF).reshape(rows, modes * 2 * coupled)
-    pi_all = lax.all_gather(pi_b, "row", axis=0, tiled=True)
+    devices_2 = lax.axis_size("row")
+    pairs = [(i, (i + 1) % devices_2) for i in range(devices_2)]
+    back = [(b_2, a_2) for a_2, b_2 in pairs]
+    lower, upper = ([], [])
+    for step in range(devices_2 - 1):
+        if step % 2 == 0:
+            lower.append(lax.ppermute(lower[-1] if lower else pi_b, "row", pairs))
+        else:
+            upper.append(lax.ppermute(upper[-1] if upper else pi_b, "row", back))
+    blocks = jnp.stack([*lower[::-1], pi_b, *upper])
+    shift = lax.axis_index("row") - len(lower)
+    blocks = blocks[(jnp.arange(devices_2) - shift) % devices_2]
+    pi_all = laid_out(blocks, 0)
     onehot = (lead_index[:, None] == jnp.arange(leads, dtype=jnp.int32)[None, :]).astype(F32)
     lam_re, lam_im = (-mode_width, mode_level)
     l_parts, m_parts = ([[], []], [[], []])

time: 599 us -> 548 us (0.915)
  waiting for transfers between devices: 329 us -> 270 us
    all_gather x1 -> x0, waiting for transfers between devices: 49.4 us -> none  [shards(): pi_all = lax.all_gather(pi_b, 'row', axis=0, tiled=True)]
    reduce_scatter x1, waiting for transfers between devices: 96.6 us -> 56.9 us  [shards(): mine = lax.psum_scatter(payload, 'mode', scatter_dimension=0, tiled=True)[0]]
    all_gather x1, waiting for transfers between devices: 41.6 us -> 71.8 us  [shards(): lax.all_gather(rho_t.reshape(2, cols, rows), 'mode', axis=1, tiled=True)]
    all_gather x1, waiting for transfers between devices: 74 us -> 53.9 us  [shards(): ham2_all = lax.all_gather(ham2_ct, 'mode', axis=0, tiled=True)]
    ppermute x0 -> x3, waiting for transfers between devices: none -> 20.1 us  [the longest x2 20.1 us: shards(): lower.append(lax.ppermute(lower[-1] if lower else pi_b, 'row', pairs))]
    unnamed x204 -> x174, local copies, waits for them, and re-layouts: 38 us -> 24.1 us
    reshape x0 -> x1, local copies, waits for them, and re-layouts: none -> 6.56 us  [laid_out(): blocks.reshape(*shape[:dim], shape[dim] * shape[dim + 1], *shape[dim + 2:])]
  transfers between devices with their start and end apart: 9 -> 11, of which waited for: 6 -> 6; matrix products, arithmetic and copies ran while one was open for 27% -> 30% of each run, Pallas kernels for 0% -> 0%
where the time goes in v1:
time: 548 us; the launch traced here: 545 us
  waiting for transfers between devices  270 us (49%)
  local copies, waits for them, and re-layouts  85.2 us (16%)
  other arithmetic  78 us (14%)
  matrix products  46.1 us (8%)
  between operations  44.8 us (8%)
  starting transfers between devices  20.3 us (4%)
    all_gather x1, waiting for transfers between devices, shards(): lax.all_gather(rho_t.reshape(2, cols, rows), 'mode', axis=1, tiled=True)  71.8 us
    all_gather x1, waiting for transfers between devices, shards(): whole = lax.all_gather(mine, 'mode', axis=0, tiled=False)  62.6 us
    reduce_scatter x1, waiting for transfers between devices, shards(): mine = lax.psum_scatter(payload, 'mode', scatter_dimension=0, tiled=True)[0]  56.9 us
    all_gather x1, waiting for transfers between devices, shards(): ham2_all = lax.all_gather(ham2_ct, 'mode', axis=0, tiled=True)  53.9 us
    dot_general x42, matrix products, dot(): lax.dot_general(a, b, (((ca,), (cb,)), ((), ())), preferred_element_type=...  46.1 us
    unnamed x174, local copies, waits for them, and re-layouts  24.1 us
    ppermute x2, waiting for transfers between devices, shards(): lower.append(lax.ppermute(lower[-1] if lower else pi_b, 'row', pairs))  20.1 us
    all_to_all x4, starting transfers between devices, over_row(): lax.all_to_all(jnp.broadcast_to(x[None], (devices, *x.shape)), 'row', 0,...  17.3 us
  transfers between devices with their start and end apart: 11, of which 6 were waited for; matrix products, arithmetic and copies ran while one was open for 30% of the time, Pallas kernels for 0%

profile of v1, /device:TPU:1, one launch (start us, length us, event | category | flops | bytes accessed | tf_op | source)
XLA Modules:
  0.0 544.9 jit_solution(5262180462119016234)
XLA Ops:
  9.8 4.8 all-to-all-start
  14.7 4.2 fusion.207
  21.2 6.2 %convert_bitcast_fusion.1 = (bf16[512,128]{1,0:T(8,128)(2,1)}, f32[512,1,1,128]{3,0,2,1:T(8,128)}, bf16[512,128]{1,0:T(8,128)(2,1)}, f32[512,1,1,128]{3,0,2,1:T(...) fusion(f32[512,1,1,128]{3,0,2,1:T(8,128)S(1)} %bitcast.356, ...), kind=kLoop, calls=%fused_computation.211 | loop fusion | flops 2097152 | bytes 3670048 | tf_op jit(solution)/shard_map/add | solution.py:92
  27.4 8.3 %add_bitcast_fusion = f32[64,8,128]{2,1,0:T(8,128)} fusion(f32[]{:T(128)} %bitcast.15, f32[]{:T(128)} %bitcast.14, f32[]{:T(128)} %bitcast.13, f32[]{:T(128)} %bitcast.12, f32[512,1,1,128]{3,0,2,1:T(8,128)S(1)} %bitcast.336, f32[]{:T(128)} %bitcast.20, f32[512,1,1,128]{3,0,2,1:T(8,128)S(1)} %bitcast.343, f32[]{:T(128)} %bitcast.19, ...), kind=kLoop, calls=%fused_computation.137 | loop fusion | flops 1245184 | bytes 2359344 | tf_op jit(solution)/shard_map/add | solution.py:99
  35.7 8.3 %add_bitcast_fusion.1 = f32[64,8,128]{2,1,0:T(8,128)} fusion(f32[]{:T(128)} %bitcast.10, f32[]{:T(128)} %bitcast.9, f32[]{:T(128)} %bitcast.8, f32[]{:T(128)} %bitcast.7, f32[512,1,1,128]{3,0,2,1:T(8,128)S(1)} %bitcast.337, f32[]{:T(128)} %bitcast.20, f32[512,1,1,128]{3,0,2,1:T(8,128)S(1)} %bitcast.344, f32[]{:T(128)} %bitcast.19, ...), kind=kLoop, calls=%fused_computation.138 | loop fusion | flops 1245184 | bytes 2359344 | tf_op jit(solution)/shard_map/add | solution.py:99
  44.1 8.4 %add_bitcast_fusion.2 = f32[64,8,128]{2,1,0:T(8,128)} fusion(f32[]{:T(128)} %bitcast.15, f32[]{:T(128)} %bitcast.14, f32[]{:T(128)} %bitcast.13, f32[]{:T(128)} %bitcast.12, f32[512,1,1,128]{3,0,2,1:T(8,128)S(1)} %bitcast.345, f32[]{:T(128)} %bitcast.20, f32[512,1,1,128]{3,0,2,1:T(8,128)S(1)} %bitcast.338, f32[]{:T(128)} %bitcast.19, ...), kind=kLoop, calls=%fused_computation.139 | loop fusion | flops 1245184 | bytes 2359344 | tf_op jit(solution)/shard_map/add | solution.py:93
  52.5 8.3 %add_bitcast_fusion.3 = f32[64,8,128]{2,1,0:T(8,128)} fusion(f32[]{:T(128)} %bitcast.10, f32[]{:T(128)} %bitcast.9, f32[]{:T(128)} %bitcast.8, f32[]{:T(128)} %bitcast.7, f32[512,1,1,128]{3,0,2,1:T(8,128)S(1)} %bitcast.346, f32[]{:T(128)} %bitcast.20, f32[512,1,1,128]{3,0,2,1:T(8,128)S(1)} %bitcast.339, f32[]{:T(128)} %bitcast.19, ...), kind=kLoop, calls=%fused_computation.140 | loop fusion | flops 1245184 | bytes 2359344 | tf_op jit(solution)/shard_map/add | solution.py:93
  63.5 1.2 convolution_negate_fusion
  64.8 1.3 fusion.83
  66.9 2.0 copy.234
  69.0 2.0 reshape.551
  71.0 2.3 pad_maximum_fusion.1
  80.8 2.6 copy.231
  84.1 13.6 %concatenate.113 = f32[64,29,512]{2,1,0:T(8,128)} concatenate(f32[64,8,512]{2,1,0:T(8,128)} %pad_maximum_fusion.1, f32[64,8,512]{2,1,0:T(8,128)} %pad_maximum_fusion.2, f32[64,8,512]{2,1,0:T(8,128)} %bitcast.391, f32[64,4,512]{2,1,0:T(4,128)} %reshape.551, f32[64,1,512]{2,1,0:T(1,128)} %scatter.8), dimensions={1} | concatenate | bytes 7602176 | tf_op jit(solution)/shard_map/concatenate | solution.py:137
  97.7 1.4 slice.1154
  100.0 3.3 convert_element_type.100
  103.2 2.6 reshape.553
  105.8 1.5 collective-permute-start
  108.5 2.6 stack_reshape.3
  142.3 1.8 fusion.205
  149.5 20.1 %collective-permute-done.1 = bf16[512,1024]{1,0:T(8,128)(2,1)S(1)} collective-permute-done((bf16[512,1024]{1,0:T(8,128)(2,1)}, bf16[512,1024]{1,0:T(8,128)(2,1)S(1)}, u32[]{:S(2)}, u32[]{:S(2)}) %collective-permute-start.1) | collective-permute-done | bytes 1048608 | tf_op jit(solution)/shard_map/ppermute | solution.py:81
  169.5 3.4 pad_maximum_fusion
  172.9 5.1 gather_fusion
  178.0 6.0 %fusion.215 = f32[1024,512]{1,0:T(8,128)} fusion(bf16[2048,1024]{1,0:T(8,128)(2,1)} %bitcast.333, bf16[512,2048]{1,0:T(8,128)(2,1)S(1)} %copy-done), kind=kOutput, calls=%fused_computation.361 | convolution fusion | flops 2147483648 | bytes 8388608 | tf_op jit(solution)/shard_map/dot_general | solution.py:18
  184.0 56.9 %reduce-scatter.2.cloned.1.call-done = f32[1,29,512]{2,1,0:T(8,128)} async-done(((f32[64,29,512]{2,1,0:T(8,128)}), f32[1,29,512]{2,1,0:T(8,128)}) %reduce-scatter.2.cloned.1.call-update) | async-done | bytes 59408 | tf_op jit(solution)/shard_map/reduce_scatter | solution.py:140
  242.2 4.0 all-to-all-start.1
  246.1 2.8 fusion.206
  249.0 6.6 %copy.241 = bf16[2048,1024]{0,1:T(8,128)(2,1)} copy(bf16[2048,1024]{1,0:T(8,128)(2,1)} %bitcast.334) | data formatting | bytes 8388608 | tf_op jit(solution)/shard_map/reshape | solution.py:14
  255.5 1.8 copy.271
  257.3 1.8 copy.270
  259.1 1.8 copy.273
  260.9 1.8 copy.272
  262.7 1.8 copy.275
  264.5 1.8 copy.274
  266.3 1.8 copy.277
  268.0 1.8 copy.276
  271.3 53.9 %all-gather.8.cloned.1.call-done = bf16[2048,512]{1,0:T(8,128)(2,1)} async-done(((bf16[32,512]{1,0:T(8,128)(2,1)}), bf16[2048,512]{1,0:T(8,128)(2,1)}) %all-gather.8.cloned.1.call-update) | async-done | bytes 2097168 | tf_op jit(solution)/shard_map/all_gather | solution.py:73
  325.2 6.5 %fusion = f32[512,4,2,128]{3,0,2,1:T(8,128)} fusion(bf16[4,2,128,2048]{3,2,1,0:T(8,128)(2,1)} %bitcast.392, bf16[2048,512]{1,0:T(8,128)(2,1)} %all-gather.8.cloned.1.call-done), kind=kOutput, calls=%fused_computation.6 | convolution fusion | flops 2147483648 | bytes 8388608 | tf_op jit(solution)/shard_map/dot_general | solution.py:18
  332.9 71.8 %all-gather.4.cloned.1.call-done = bf16[2,2048,512]{2,1,0:T(8,128)(2,1)} async-done(((bf16[2,32,512]{2,1,0:T(8,128)(2,1)}), bf16[2,2048,512]{2,1,0:T(8,128)(2,1)}) %all-gather.4.cloned.1.call-update) | async-done | bytes 4194320 | tf_op jit(solution)/shard_map/all_gather | solution.py:72
  404.7 3.0 fusion.10
  407.7 2.9 select_subtract_fusion.1
  410.6 2.0 multiply_subtract_fusion.1
  412.6 2.9 select_subtract_fusion
  415.5 1.5 select_subtract_fusion.5
  419.2 62.6 %all-gather.6.cloned.1.call-done = bf16[64,28,512]{2,1,0:T(8,128)(2,1)} async-done(((bf16[1,28,512]{2,1,0:T(8,128)(2,1)}), bf16[64,28,512]{2,1,0:T(8,128)(2,1)}) %all-gather.6.cloned.1.call-update) | async-done | bytes 1835024 | tf_op jit(solution)/shard_map/all_gather | solution.py:144
  483.5 1.5 fusion.23
  491.5 4.3 all-to-all-start.2
  495.8 1.8 slice.782
  497.7 1.7 reshape.556
  499.4 1.9 fusion.8
  501.9 2.7 fusion.78
  504.6 1.3 fusion.72
  506.0 1.5 fusion.66
  507.6 1.6 fusion.60
  509.2 1.5 fusion.54
  510.7 1.4 fusion.48
  512.2 1.5 fusion.42
  513.7 1.4 fusion.36
  515.1 2.9 copy.252
  518.0 1.3 convolution_convert_fusion.5
  521.0 4.2 all-to-all-start.3
  526.1 1.7 slice_bitcast_fusion.15
  527.8 4.5 all-to-all-done.3
  533.4 2.4 fusion.6
  (268 shorter events, 46.0 us)
Async XLA Ops:
  7.2 7.5 %copy-start.44 = (f32[2,512,32]{1,2,0:T(8,128)S(1)}, f32[2,512,32]{1,2,0:T(8,128)}, u32[]{:S(2)}) copy-start(f32[2,512,32]{1,2,0:T(8,128)} %param.12) | copy-start | bytes 393220
  9.8 65.4 %all-to-all-start = ((bf16[4,96,512]{2,1,0:T(8,128)(2,1)}), bf16[4,96,512]{2,1,0:T(8,128)(2,1)}, u32[]{:S(2)}, u32[]{:S(2)}) async-start(bf16[4,96,512]{2,1,0:T(8,128)(2,1)} %broadcast_in_dim.18), calls=%async_computation | async-start | bytes 786432 | tf_op jit(solution)/shard_map/all_to_all | solution.py:23
  14.7 226.2 %reduce-scatter.2.cloned.1.call-start = ((), (), s32[]{:S(2)}) async-start(), calls=%async_computation.6 | async-start | bytes 4259840 | tf_op jit(solution)/shard_map/reduce_scatter | solution.py:140
  14.7 59.9 %copy-start.41 = (bf16[2,32,512]{2,1,0:T(8,128)(2,1)}, bf16[2,32,512]{2,1,0:T(8,128)(2,1)S(1)}, u32[]{:S(2)}) copy-start(bf16[2,32,512]{2,1,0:T(8,128)(2,1)S(1)} %convert_bitcast_fusion.5) | copy-start | bytes 196612
  14.7 4.3 copy-start.75
  14.7 5.2 copy-start.74
  14.7 5.8 %copy-start.78 = (f32[4]{0:T(128)S(1)}, f32[4]{0:T(128)}, u32[]{:S(2)}) copy-start(f32[4]{0:T(128)} %param.18) | copy-start | bytes 52
  18.9 33.5 %copy-start.1 = (f32[512,1,1,128]{3,2,1,0:T(1,128)}, f32[512,1,1,128]{3,2,1,0:T(1,128)S(1)}, u32[]{:S(2)}) copy-start(f32[512,1,1,128]{3,2,1,0:T(1,128)S(1)} %get-tuple-element.63) | copy-start | bytes 786436
  19.0 33.5 %copy-start.3 = (f32[512,1,1,128]{3,2,1,0:T(1,128)}, f32[512,1,1,128]{3,2,1,0:T(1,128)S(1)}, u32[]{:S(2)}) copy-start(f32[512,1,1,128]{3,2,1,0:T(1,128)S(1)} %get-tuple-element.60) | copy-start | bytes 786436
  19.0 33.5 %copy-start.5 = (f32[512,1,1,128]{3,2,1,0:T(1,128)}, f32[512,1,1,128]{3,2,1,0:T(1,128)S(1)}, u32[]{:S(2)}) copy-start(f32[512,1,1,128]{3,2,1,0:T(1,128)S(1)} %get-tuple-element.64) | copy-start | bytes 786436
  44.1 17.3 %copy-start.58 = (s32[2,128]{1,0:T(2,128)S(1)}, s32[2,128]{1,0:T(2,128)}, u32[]{:S(2)}) copy-start(s32[2,128]{1,0:T(2,128)} %param.15) | copy-start | bytes 3076
  44.1 17.4 %copy-start.26 = (bf16[2,128,128]{2,1,0:T(8,128)(2,1)S(1)}, bf16[2,128,128]{2,1,0:T(8,128)(2,1)}, u32[]{:S(2)}) copy-start(bf16[2,128,128]{2,1,0:T(8,128)(2,1)} %param.21) | copy-start | bytes 196612
  64.8 6.2 %copy-start.64 = (f32[4,2]{0,1:T(2,128)S(1)}, f32[4,2]{0,1:T(2,128)}, u32[]{:S(2)}) copy-start(f32[4,2]{0,1:T(2,128)} %param.19) | copy-start | bytes 100
  64.8 6.2 %copy-start.73 = (f32[4]{0:T(128)S(1)}, f32[4]{0:T(128)}, u32[]{:S(2)}) copy-start(f32[4]{0:T(128)} %param.20) | copy-start | bytes 52
  70.9 2.4 copy-start.29
  70.9 2.4 copy-start.30
  70.9 2.4 copy-start.31
  70.9 2.4 copy-start.32
  76.2 2.7 copy-start.68
  76.2 2.7 copy-start.69
  76.9 2.5 copy-start.51
  97.7 227.5 %all-gather.8.cloned.1.call-start = ((), (), s32[]{:S(2)}) async-start(), calls=%async_computation.8 | async-start | bytes 2129920 | tf_op jit(solution)/shard_map/all_gather | solution.py:73
  99.2 305.4 %all-gather.4.cloned.1.call-start = ((), (), s32[]{:S(2)}) async-start(), calls=%async_computation.5 | async-start | bytes 4259840 | tf_op jit(solution)/shard_map/all_gather | solution.py:72
  105.8 40.7 %collective-permute-start = (bf16[512,1024]{1,0:T(8,128)(2,1)}, bf16[512,1024]{1,0:T(8,128)(2,1)}, u32[]{:S(2)}, u32[]{:S(2)}) collective-permute-start(bf16[512,1024]{1,0:T(8,128)(2,1)} %reshape.553), channel_id=1, source_target_pairs={{0,1},{1,2},{2,3},{3,0},{4,5},{5,6},{6,7},{7,4},{8,9},{9,10},{10,1... | collective-permute-start | bytes 3145736 | tf_op jit(solution)/shard_map/ppermute | solution.py:81
  107.3 42.2 %collective-permute-start.2 = (bf16[512,1024]{1,0:T(8,128)(2,1)}, bf16[512,1024]{1,0:T(8,128)(2,1)}, u32[]{:S(2)}, u32[]{:S(2)}) collective-permute-start(bf16[512,1024]{1,0:T(8,128)(2,1)} %reshape.553), channel_id=1, source_target_pairs={{1,0},{2,1},{3,2},{0,3},{5,4},{6,5},{7,6},{4,7},{9,8},{10,9},{11,1... | collective-permute-start | bytes 3145736 | tf_op jit(solution)/shard_map/ppermute | solution.py:83
  144.9 24.6 %copy-start.11 = (bf16[1,512,1024]{2,1,0:T(8,128)(2,1)S(1)}, bf16[1,512,1024]{2,1,0:T(8,128)(2,1)}, u32[]{:S(2)}) copy-start(bf16[1,512,1024]{2,1,0:T(8,128)(2,1)} %stack_reshape.3) | copy-start | bytes 3145732
  146.5 23.0 %collective-permute-start.1 = (bf16[512,1024]{1,0:T(8,128)(2,1)}, bf16[512,1024]{1,0:T(8,128)(2,1)S(1)}, u32[]{:S(2)}, u32[]{:S(2)}) collective-permute-start(bf16[512,1024]{1,0:T(8,128)(2,1)} %collective-permute-done), channel_id=1, source_target_pairs={{0,1},{1,2},{2,3},{3,0},{4,5},{5,6},{6,7},{7,4},{8,9},{9,10},{10,1... | collective-permute-start | bytes 3145736 | tf_op jit(solution)/shard_map/ppermute | solution.py:81
  242.2 28.5 %all-to-all-start.1 = ((f32[4,4,512]{2,1,0:T(4,128)}), f32[4,4,512]{2,1,0:T(4,128)S(1)}, u32[]{:S(2)}, u32[]{:S(2)}) async-start(f32[4,4,512]{2,1,0:T(4,128)} %broadcast_in_dim.20), calls=%async_computation.2 | async-start | bytes 65536 | tf_op jit(solution)/shard_map/all_to_all | solution.py:23
  246.1 235.7 %all-gather.6.cloned.1.call-start = ((), (), s32[]{:S(2)}) async-start(), calls=%async_computation.7 | async-start | bytes 2129920 | tf_op jit(solution)/shard_map/all_gather | solution.py:144
  404.6 3.0 copy-start.9
  404.6 5.9 %copy-start.55 = (bf16[512,128]{1,0:T(8,128)(2,1)S(1)}, bf16[512,128]{1,0:T(8,128)(2,1)}, u32[]{:S(2)}) copy-start(bf16[512,128]{1,0:T(8,128)(2,1)} %copy-done.54) | copy-start | bytes 393220
  404.6 5.9 %copy-start.57 = (bf16[512,128]{1,0:T(8,128)(2,1)S(1)}, bf16[512,128]{1,0:T(8,128)(2,1)}, u32[]{:S(2)}) copy-start(bf16[512,128]{1,0:T(8,128)(2,1)} %copy-done.56) | copy-start | bytes 393220
  404.7 5.9 %copy-start.76 = (bf16[2,2048,512]{2,1,0:T(8,128)(2,1)S(1)}, bf16[2,2048,512]{2,1,0:T(8,128)(2,1)}, u32[]{:S(2)}) copy-start(bf16[2,2048,512]{2,1,0:T(8,128)(2,1)} %all-gather.4.cloned.1.call-done) | copy-start | bytes 12582916
  404.7 5.9 %copy-start.79 = (bf16[2048,128]{0,1:T(8,128)(2,1)S(1)}, bf16[2048,128]{0,1:T(8,128)(2,1)}, u32[]{:S(2)}) copy-start(bf16[2048,128]{0,1:T(8,128)(2,1)} %convolution_convert_fusion) | copy-start | bytes 1572868
  404.7 5.9 %copy-start.80 = (bf16[2048,128]{0,1:T(8,128)(2,1)S(1)}, bf16[2048,128]{0,1:T(8,128)(2,1)}, u32[]{:S(2)}) copy-start(bf16[2048,128]{0,1:T(8,128)(2,1)} %convolution_convert_fusion.1) | copy-start | bytes 1572868
  412.6 4.4 copy-start.50
  418.1 64.9 %copy-start.71 = (s32[32]{0:T(128)S(1)}, s32[32]{0:T(128)}, u32[]{:S(2)}) copy-start(s32[32]{0:T(128)} %copy-done.70) | copy-start | bytes 388
  419.2 66.5 %copy-start.59 = (s32[2,128]{1,0:T(2,128)S(1)}, s32[2,128]{1,0:T(2,128)}, u32[]{:S(2)}) copy-start(s32[2,128]{1,0:T(2,128)} %param.15) | copy-start | bytes 3076
  483.0 6.1 %copy-start.7 = (bf16[512,512]{1,0:T(8,128)(2,1)}, bf16[512,512]{1,0:T(8,128)(2,1)S(1)}, u32[]{:S(2)}) copy-start(bf16[512,512]{1,0:T(8,128)(2,1)S(1)} %slice_bitcast_fusion.14) | copy-start | bytes 1572868
  483.4 6.6 %copy-start.40 = (f32[96,512]{1,0:T(8,128)S(1)}, f32[96,512]{1,0:T(8,128)}, u32[]{:S(2)}) copy-start(f32[96,512]{1,0:T(8,128)} %copy-done.39) | copy-start | bytes 589828
  483.4 6.6 %copy-start.62 = (f32[32,512]{1,0:T(8,128)S(1)}, f32[32,512]{1,0:T(8,128)}, u32[]{:S(2)}) copy-start(f32[32,512]{1,0:T(8,128)} %fusion.7) | copy-start | bytes 196612
  483.5 6.6 %copy-start.63 = (f32[32,512]{1,0:T(8,128)S(1)}, f32[32,512]{1,0:T(8,128)}, u32[]{:S(2)}) copy-start(f32[32,512]{1,0:T(8,128)} %fusion.4) | copy-start | bytes 196612
  483.5 7.3 %copy-start.46 = (bf16[32,512]{1,0:T(8,128)(2,1)S(1)}, bf16[32,512]{1,0:T(8,128)(2,1)}, u32[]{:S(2)}) copy-start(bf16[32,512]{1,0:T(8,128)(2,1)} %slice.1154) | copy-start | bytes 98308
  485.0 5.0 copy-start.23
  487.4 12.0 %copy-start.66 = (s32[512]{0:T(512)S(1)}, s32[512]{0:T(512)}, u32[]{:S(2)}) copy-start(s32[512]{0:T(512)} %copy-done.65) | copy-start | bytes 6148
  491.5 28.7 %all-to-all-start.2 = ((bf16[4,96,512]{2,1,0:T(8,128)(2,1)}), bf16[4,96,512]{2,1,0:T(8,128)(2,1)}, u32[]{:S(2)}, u32[]{:S(2)}) async-start(bf16[4,96,512]{2,1,0:T(8,128)(2,1)} %broadcast_in_dim.21), calls=%async_computation.3 | async-start | bytes 786432 | tf_op jit(solution)/shard_map/all_to_all | solution.py:23
  499.4 2.5 copy-start.25
  499.4 2.5 copy-start.27
  501.9 4.1 copy-start.4
  501.9 4.1 copy-start.6
  501.9 4.1 copy-start.21
  501.9 4.1 copy-start.22
  501.9 4.1 copy-start.37
  501.9 4.1 copy-start.38
  515.1 4.3 copy-start.53
  515.1 4.3 copy-start.24
  515.1 4.3 copy-start.60
  515.1 4.3 copy-start.72
  518.0 14.3 %copy-start.16 = (bf16[256,512]{1,0:T(8,128)(2,1)S(1)}, bf16[256,512]{1,0:T(8,128)(2,1)}, u32[]{:S(2)}) copy-start(bf16[256,512]{1,0:T(8,128)(2,1)} %copy-done.14) | copy-start | bytes 786436
  519.4 13.3 %copy-start.8 = (bf16[512,512]{1,0:T(8,128)(2,1)S(1)}, bf16[512,512]{1,0:T(8,128)(2,1)}, u32[]{:S(2)}) copy-start(bf16[512,512]{1,0:T(8,128)(2,1)} %copy-done.7) | copy-start | bytes 1572868
  521.0 11.2 %all-to-all-start.3 = ((bf16[4,96,512]{2,1,0:T(8,128)(2,1)}), bf16[4,96,512]{2,1,0:T(8,128)(2,1)S(1)}, u32[]{:S(2)}, u32[]{:S(2)}) async-start(bf16[4,96,512]{2,1,0:T(8,128)(2,1)} %broadcast_in_dim.26), calls=%async_computation.4 | async-start | bytes 786432 | tf_op jit(solution)/shard_map/all_to_all | solution.py:23
  532.5 3.3 copy-start.77
  533.4 2.9 copy-start.47
  533.4 2.9 copy-start.48
  (28 other events, 41.1 us)
Sparse Core Ops, SparseCore 0:
  97.8 142.9 reduce-scatter.1
  243.6 81.5 all-gather.7
  328.0 76.6 all-gather.3
  407.3 74.4 all-gather.5
